TPU v7x, 256 devices: a whole 4x4x8 slice. The times are simulated.
256 devices in a mesh: seq: 64 (over y, z, core), tp: 4 (over x).
Axes of the slice: x: 4, y: 4, z: 8, core: 2. Of those that a mesh axis runs over, the one named last changes fastest.
Arguments:
- tokens: bfloat16 [49152, 4096], P('seq'), may hold values from -6 to 6
- query_weight: bfloat16 [4096, 2048], P('seq', 'tp'), may hold values from -0.09375 to 0.09375
- key_weight: bfloat16 [4096, 2048], P('seq', 'tp'), may hold values from -0.09375 to 0.09375
- value_weight: bfloat16 [4096, 2048], P('seq', 'tp'), may hold values from -0.09375 to 0.09375
- gate_weight: bfloat16 [4096, 16], P('seq', 'tp'), may hold values from -0.09375 to 0.09375
- decay_rate: float32 [16], P('tp'), may hold values from 4.0690106e-06 to 0.04
- norm_gain: float32 [2048], P('tp'), may hold values from 0.5 to 1.5
- out_weight: bfloat16 [2048, 4096], P(None, 'tp'), may hold values from -0.125 to 0.125
Outputs:
- mixed: bfloat16 [49152, 4096], P('seq', 'tp')
All inputs are finite; a program needn't handle non-finite values.
Results may differ from a plain program's by a relative error of at most 0.006.
The roundings to bfloat16 on the way count: a program that leaves them out, or rounds other values in their place, can miss the bound.
Values may be sent and summed in bfloat16 or wider, within the bound.
A program may use at most 128 MiB of HBM per device.

v0:
```python
import jax
import jax.numpy as jnp
from jax import lax
from jax.sharding import Mesh
from jax.sharding import PartitionSpec as P

SEQ = ("seq_0", "seq_1", "seq_2")


def side_by_side(arrays, axis, dim, along):
    both = jnp.concatenate(arrays, axis=along)
    whole, at, finished = (lax.all_gather(both, axis, axis=dim, tiled=True), 0, [])
    for a in arrays:
        finished.append(lax.slice_in_dim(whole, at, at + a.shape[along], axis=along))
        at += a.shape[along]
    return tuple(finished)


def nothing_yet(shard, identity):
    return jax.tree.map(
        lambda part, zero: jnp.zeros_like(part) + jnp.asarray(zero, part.dtype), shard, identity
    )


def carried_in(shard, axes, combine, identity):
    before = start = nothing_yet(shard, identity)
    so_far = shard
    for axis in reversed(axes):
        peers, position = (lax.axis_size(axis), lax.axis_index(axis))
        pieces = jax.tree.map(lambda part: lax.all_gather(part, axis), so_far)
        inside, so_far = (start, start)
        for k in range(peers):
            passed = k < position
            so_far = combine(so_far, jax.tree.map(lambda part: part[k], pieces))
            inside = jax.tree.map(lambda new, old: jnp.where(passed, new, old), so_far, inside)
        before = combine(inside, before)
    return before


def on_device(
    tokens, query_weight, key_weight, value_weight, gate_weight, decay_rate, norm_gain, out_weight
):
    tok_rows = tokens.shape[0]
    head_count = decay_rate.shape[0]
    proj_width = query_weight.shape[1]
    head_size = proj_width // head_count

    def contract(piece):
        return jnp.dot(tokens, piece, preferred_element_type=jnp.float32)

    pieces = side_by_side((query_weight, key_weight, value_weight, gate_weight), SEQ, 0, 1)
    query_proj, key_proj, value_proj, gate_logit = tuple(
        (contract(one_piece) for one_piece in pieces)
    )
    query_heads = query_proj.astype(jnp.bfloat16).reshape(tok_rows, head_count, head_size)
    key_heads = key_proj.astype(jnp.bfloat16).reshape(tok_rows, head_count, head_size)
    value_per_head = value_proj.astype(jnp.bfloat16).reshape(tok_rows, head_count, head_size)
    log_decay = -decay_rate[None, :] * jax.nn.softplus(gate_logit)
    within = jnp.cumsum(log_decay, axis=0)
    block_total = within[-1]
    key_scaled = (jnp.exp(block_total[None, :] - within)[:, :, None] * key_heads).astype(
        jnp.bfloat16
    )
    shard_local_state = jnp.einsum(
        "gfw,gfz->fwz", key_scaled, value_per_head, preferred_element_type=jnp.float32
    )

    def decayed_join(earlier, later):
        return (earlier[0] + later[0], jnp.exp(later[0])[:, None, None] * earlier[1] + later[1])

    _, prefix_state = carried_in(
        (block_total, shard_local_state),
        SEQ,
        decayed_join,
        (jnp.zeros_like(block_total), jnp.zeros_like(shard_local_state)),
    )
    query_scaled = (jnp.exp(within)[:, :, None] * query_heads).astype(jnp.bfloat16)
    carried_state = jnp.einsum(
        "fys,ysu->fyu",
        query_scaled,
        prefix_state.astype(jnp.bfloat16),
        preferred_element_type=jnp.float32,
    )
    scores = jnp.einsum("thk,shk->hts", query_heads, key_heads, preferred_element_type=jnp.float32)
    row_index = lax.broadcasted_iota(jnp.int32, (tok_rows, tok_rows), 0)
    col_index = lax.broadcasted_iota(jnp.int32, (tok_rows, tok_rows), 1)
    causal = (col_index <= row_index)[None, :, :]
    decay_gap = within.T[:, :, None] - within.T[:, None, :]
    attn = jnp.where(causal, scores * jnp.exp(jnp.where(causal, decay_gap, 0.0)), 0.0).astype(
        jnp.bfloat16
    )
    local_part = jnp.einsum(
        "hts,shv->thv", attn, value_per_head, preferred_element_type=jnp.float32
    )
    head_out = carried_state + local_part
    mean_square = jnp.mean(head_out * head_out, axis=-1, keepdims=True)
    normed = (head_out * lax.rsqrt(mean_square + 1e-05)).reshape(tok_rows, proj_width) * norm_gain[
        None, :
    ]
    normed = normed.astype(jnp.bfloat16)
    mixed = jnp.dot(
        lax.all_gather(normed, "tp", axis=1, tiled=True),
        out_weight,
        preferred_element_type=jnp.float32,
    )
    return mixed.astype(jnp.bfloat16)


def solution(mesh):
    finer = Mesh(mesh.devices.reshape(4, 8, 2, mesh.shape["tp"]), ("seq_0", "seq_1", "seq_2", "tp"))
    return jax.shard_map(
        on_device,
        mesh=finer,
        in_specs=(
            P(SEQ, None),
            P(SEQ, "tp"),
            P(SEQ, "tp"),
            P(SEQ, "tp"),
            P(SEQ, "tp"),
            P("tp"),
            P("tp"),
            P(None, "tp"),
        ),
        out_specs=P(SEQ, "tp"),
        check_vma=False,
    )
```

profile of v0, /device:TPU:1, one launch (start us, length us, event | category | flops | bytes accessed | tf_op | source)
XLA Modules:
  0.0 258.8 jit_solution(4576178796495780604)
XLA Ops:
  6.5 0.8 copy.26
  7.3 1.6 pad_maximum_fusion
  9.0 0.7 neg.9
  9.7 96.5 %all-gather.9.cloned.1.call-done = bf16[4096,1540]{1,0:T(8,128)(2,1)} async-done(((bf16[64,1540]{1,0:T(8,128)(2,1)}), bf16[4096,1540]{1,0:T(8,128)(2,1)}) %all-gather.9.cloned.1.call-update) | async-done | bytes 12615696 | tf_op jit(solution)/shard_map/all_gather | solution.py:12
  106.2 5.0 %fusion.70 = f32[4,768]{1,0:T(4,128)S(1)} fusion(bf16[768,4096]{1,0:T(8,128)(2,1)} %param.8, bf16[4096,1540]{1,0:T(8,128)(2,1)} %all-gather.9.cloned.1.call-done, f32[4]{0:T(128)S(1)} %neg.9), kind=kOutput, calls=%fused_computation.90 | convolution fusion | flops 25187328 | bytes 7352336 | tf_op jit(solution)/shard_map/dot_general | solution.py:49
  111.2 1.1 reduce-window.6
  113.1 7.7 %fusion.15 = bf16[512,768]{1,0:T(8,128)(2,1)S(1)} fusion(bf16[768,4096]{1,0:T(8,128)(2,1)} %param.8, bf16[4096,1540]{1,0:T(8,128)(2,1)} %all-gather.9.cloned.1.call-done), kind=kOutput, calls=%fused_computation.21 | convolution fusion | flops 3221618688 | bytes 11272192 | tf_op jit(solution)/shard_map/dot_general | solution.py:49
  120.8 5.9 %fusion.12 = bf16[512,768]{1,0:T(8,128)(2,1)S(1)} fusion(bf16[768,4096]{1,0:T(8,128)(2,1)S(1)} %bitcast.238, bf16[4096,1540]{1,0:T(8,128)(2,1)} %all-gather.9.cloned.1.call-done), kind=kOutput, calls=%fused_computation.20 | convolution fusion | flops 3221618688 | bytes 11272192 | tf_op jit(solution)/shard_map/dot_general | solution.py:49
  126.8 0.4 fusion.23
  127.1 2.2 all-gather
  129.3 1.8 all-gather.1
  131.1 0.8 bitcast_add_fusion.8
  132.2 11.1 %all-gather.2 = f32[8,1,4]{2,1,0:T(1,128)S(1)} all-gather(f32[1,1,4]{2,1,0:T(1,128)S(1)} %get-tuple-element.23), channel_id=1, replica_groups=mesh['seq_0'=4,'seq_1'=8,'seq_2'=2,'tp'=4] {'seq_1'}, dimensions={0}, use_global_device_ids=true | all-gather | bytes 144 | tf_op jit(solution)/shard_map/all_gather | solution.py:30
  143.4 22.0 %all-gather.11.cloned.1.call-done = f32[8,4,128,128]{3,2,1,0:T(8,128)} async-done(((f32[1,4,128,128]{3,2,1,0:T(8,128)}), f32[8,4,128,128]{3,2,1,0:T(8,128)}) %all-gather.11.cloned.1.call-update) | async-done | bytes 2097168 | tf_op jit(solution)/shard_map/all_gather | solution.py:30
  165.4 2.4 multiply_add_fusion
  168.0 7.5 %fusion.18 = bf16[512,768]{1,0:T(8,128)(2,1)S(1)} fusion(bf16[768,4096]{1,0:T(8,128)(2,1)} %param.8, bf16[4096,1540]{1,0:T(8,128)(2,1)} %all-gather.9.cloned.1.call-done), kind=kOutput, calls=%fused_computation.22 | convolution fusion | flops 3221618688 | bytes 11272192 | tf_op jit(solution)/shard_map/dot_general | solution.py:49
  175.6 7.7 %all-gather.3 = f32[4,1,4]{2,1,0:T(1,128)S(1)} all-gather(f32[1,1,4]{2,1,0:T(1,128)S(1)} %get-tuple-element.10), channel_id=1, replica_groups=mesh['seq_0'=4,'seq_1'=8,'seq_2'=2,'tp'=4] {'seq_0'}, dimensions={0}, use_global_device_ids=true | all-gather | bytes 80 | tf_op jit(solution)/shard_map/all_gather | solution.py:30
  183.2 0.4 copy.28
  183.7 6.7 %fusion = f32[4,128,768]{2,1,0:T(8,128)} fusion(bf16[768,4,128]{0,2,1:T(8,128)(2,1)} %bitcast.245, f32[4,768]{1,0:T(4,128)S(1)} %get-tuple-element.9, pred[768,768]{1,0:T(8,128)(4,1)S(1)} %iota_compare_fusion, bf16[768,4,128]{0,2,1:T(8,128)(2,1)S(1)} %bitcast.240, bf16[768,4,128]{0,2,1:T(8,128)(2,1)} %bitcast.247), kind=kOutput, calls=%fused_computation.1 | convolution fusion | flops 1219756032 | bytes 4534272 | tf_op jit(solution)/shard_map/hts,shv->thv/dot_general | solution.py:92
  190.3 5.0 %all-gather.13.cloned.1.call-done = f32[4,4,128,128]{3,2,1,0:T(8,128)} async-done(((f32[1,4,128,128]{3,2,1,0:T(8,128)}), f32[4,4,128,128]{3,2,1,0:T(8,128)}) %all-gather.13.cloned.1.call-update) | async-done | bytes 1048592 | tf_op jit(solution)/shard_map/all_gather | solution.py:30
  195.3 3.5 %fusion.11 = (f32[768,4]{0,1:T(4,128)S(1)}, f32[4,128,768]{2,1,0:T(8,128)S(1)}) fusion(f32[4,128,768]{2,1,0:T(8,128)} %fusion, bf16[768,4,128]{2,0,1:T(8,128)(2,1)S(1)} %copy.28, f32[768,4]{0,1:T(4,128)S(1)} %get-tuple-element.8, f32[4,4,128,128]{3,2,1,0:T(8,128)} %all-gather.13.cloned.1.call-done, f32[8,4,128,128]{3,2,1,0:T(8,128)} %all-gather.11.cloned.1.call-done, ...), kind=kOutput, calls=%fused_computation.16 | convolution fusion | flops 105903104 | bytes 7627022 | tf_op jit(solution)/shard_map/fys,ysu->fyu/dot_general | solution.py:78
  199.0 1.0 fusion.10
  200.1 44.4 %all-gather.15.cloned.1.call-done = bf16[768,2048]{0,1:T(8,128)(2,1)} async-done(((bf16[768,512]{0,1:T(8,128)(2,1)}), bf16[768,2048]{0,1:T(8,128)(2,1)}) %all-gather.15.cloned.1.call-update) | async-done | bytes 3145744 | tf_op jit(solution)/shard_map/all_gather | solution.py:102
  244.5 7.8 %convolution_convert_fusion = bf16[768,1024]{1,0:T(8,128)(2,1)} fusion(bf16[768,2048]{0,1:T(8,128)(2,1)} %all-gather.15.cloned.1.call-done, bf16[2048,1024]{1,0:T(8,128)(2,1)} %param.15), kind=kOutput, calls=%fused_computation.11 | convolution fusion | flops 3222011904 | bytes 8912896 | tf_op jit(solution)/shard_map/dot_general | solution.py:101
  (35 shorter events, 1.5 us)
Async XLA Ops:
  6.5 99.7 %all-gather.9.cloned.1.call-start = ((), (), s32[]{:S(2)}) async-start(), calls=%async_computation | async-start | bytes 13844480 | tf_op jit(solution)/shard_map/all_gather | solution.py:12
  8.9 156.4 %all-gather.11.cloned.1.call-start = ((), (), s32[]{:S(2)}) async-start(), calls=%async_computation.1 | async-start | bytes 2359296 | tf_op jit(solution)/shard_map/all_gather | solution.py:30
  106.2 14.6 %slice-start = ((s8[6291456]{0:T(1024)(128)(4,1)}), s8[2097152]{0:T(1024)(128)(4,1)S(1)}, s32[]{:S(2)}) async-start(s8[6291456]{0:T(1024)(128)(4,1)} %bitcast.237), calls=%async_computation.4 | async-start | bytes 4194304
  113.1 7.7 %slice-start.1 = ((s8[6291456]{0:T(1024)(128)(4,1)}), s8[4194304]{0:T(1024)(128)(4,1)S(1)}, s32[]{:S(2)}) async-start(s8[6291456]{0:T(1024)(128)(4,1)} %bitcast.237), calls=%async_computation.5 | async-start | bytes 8388608
  120.8 6.0 %copy-start.1 = (bf16[512,768]{1,0:T(8,128)(2,1)}, bf16[512,768]{1,0:T(8,128)(2,1)S(1)}, u32[]{:S(2)}) copy-start(bf16[512,768]{1,0:T(8,128)(2,1)S(1)} %fusion.15) | copy-start | bytes 2359300
  126.7 4.4 %copy-start.2 = (bf16[512,768]{1,0:T(8,128)(2,1)}, bf16[512,768]{1,0:T(8,128)(2,1)S(1)}, u32[]{:S(2)}) copy-start(bf16[512,768]{1,0:T(8,128)(2,1)S(1)} %fusion.12) | copy-start | bytes 2359300
  131.9 63.4 %all-gather.13.cloned.1.call-start = ((), (), s32[]{:S(2)}) async-start(), calls=%async_computation.2 | async-start | bytes 1310720 | tf_op jit(solution)/shard_map/all_gather | solution.py:30
  167.8 76.7 %all-gather.15.cloned.1.call-start = ((), (), s32[]{:S(2)}) async-start(), calls=%async_computation.3 | async-start | bytes 3932160 | tf_op jit(solution)/shard_map/all_gather | solution.py:102
  195.3 3.7 %copy-start = (f32[512]{0:T(512)S(1)}, f32[512]{0:T(512)}, u32[]{:S(2)}) copy-start(f32[512]{0:T(512)} %param.14) | copy-start | bytes 6148
Sparse Core Ops, SparseCore 0:
  10.1 96.0 all-gather.8
  132.1 33.2 all-gather.10
  167.9 27.3 all-gather.12
  200.2 44.2 all-gather.14
where the time goes:
time: 259 us
  waiting for transfers between devices  168 us (65%)
  matrix products  44.5 us (17%)
  blocking collectives  22.8 us (9%)
  between operations  13.3 us (5%)
  other arithmetic  8.38 us (3%)
    all_gather x1, waiting for transfers between devices, side_by_side(): lax.all_gather(both, axis, axis=dim, tiled=True)  96.5 us
    all_gather x1, waiting for transfers between devices, on_device(): lax.all_gather(normed, 'tp', axis=1, tiled=True)  44.4 us
    all_gather x2, waiting for transfers between devices, carried_in(): pieces = jax.tree.map(lambda part: lax.all_gather(part, axis), so_far)  27 us
    dot_general x4, matrix products, contract(): return jnp.dot(tokens, piece, preferred_element_type=jnp.float32)  26.1 us
    all_gather x4, blocking collectives, carried_in(): pieces = jax.tree.map(lambda part: lax.all_gather(part, axis), so_far)  22.8 us
    dot_general x1, matrix products, on_device(): jnp.dot(lax.all_gather(normed, 'tp', axis=1, tiled=True), out_weight, pre...  7.75 us
    dot_general x1, matrix products, on_device(): jnp.einsum('hts,shv->thv', attn, value_per_head, preferred_element_type=j...  6.66 us
  transfers between devices with their start and end apart: 4, of which 4 were waited for; matrix products, arithmetic and copies ran while one was open for 6% of the time, Pallas kernels for 0%

commit v1 on v0

--- a/solution.py
+++ b/solution.py
@@ -3,6 +3,7 @@
 from jax import lax
 from jax.sharding import Mesh
 from jax.sharding import PartitionSpec as P
+from jax.lax import all_gather
 
 SEQ = ("seq_0", "seq_1", "seq_2")
 
@@ -99,7 +100,7 @@
     ]
     normed = normed.astype(jnp.bfloat16)
     mixed = jnp.dot(
-        lax.all_gather(normed, "tp", axis=1, tiled=True),
+        jnp.concatenate(all_gather(normed, "tp"), axis=1),
         out_weight,
         preferred_element_type=jnp.float32,
     )

time: 259 us -> 262 us (1.012)
  local copies, waits for them, and re-layouts: 1.55 us -> 5.25 us
    all_gather x0 -> x1, local copies, waits for them, and re-layouts: none -> 3.18 us  [on_device(): all_gather(normed, 'tp')]
where the time goes in v1:
time: 262 us
  waiting for transfers between devices  168 us (64%)
  matrix products  43.4 us (17%)
  blocking collectives  22.8 us (9%)
  between operations  13.4 us (5%)
  other arithmetic  8.4 us (3%)
  local copies, waits for them, and re-layouts  5.25 us (2%)
    all_gather x1, waiting for transfers between devices, side_by_side(): lax.all_gather(both, axis, axis=dim, tiled=True)  96.5 us
    all_gather x1, waiting for transfers between devices, on_device(): all_gather(normed, 'tp')  44.4 us
    all_gather x2, waiting for transfers between devices, carried_in(): pieces = jax.tree.map(lambda part: lax.all_gather(part, axis), so_far)  27 us
    dot_general x4, matrix products, contract(): return jnp.dot(tokens, piece, preferred_element_type=jnp.float32)  26.1 us
    all_gather x4, blocking collectives, carried_in(): pieces = jax.tree.map(lambda part: lax.all_gather(part, axis), so_far)  22.8 us
    dot_general x1, matrix products, on_device(): jnp.dot(jnp.concatenate(all_gather(normed, 'tp'), axis=1), out_weight, pr...  6.76 us
    dot_general x1, matrix products, on_device(): jnp.einsum('hts,shv->thv', attn, value_per_head, preferred_element_type=j...  6.62 us
  transfers between devices with their start and end apart: 4, of which 4 were waited for; matrix products, arithmetic and copies ran while one was open for 6% of the time, Pallas kernels for 0%

profile of v1, /device:TPU:1, one launch (start us, length us, event | category | flops | bytes accessed | tf_op | source)
XLA Modules:
  0.0 261.5 jit_solution(9293480194204215606)
XLA Ops:
  6.5 0.8 copy.33
  7.3 1.6 pad_maximum_fusion
  9.0 0.7 neg.9
  9.7 96.5 %all-gather.9.cloned.1.call-done = bf16[4096,1540]{1,0:T(8,128)(2,1)} async-done(((bf16[64,1540]{1,0:T(8,128)(2,1)}), bf16[4096,1540]{1,0:T(8,128)(2,1)}) %all-gather.9.cloned.1.call-update) | async-done | bytes 12615696 | tf_op jit(solution)/shard_map/all_gather | solution.py:13
  106.2 5.0 %fusion.69 = f32[4,768]{1,0:T(4,128)S(1)} fusion(bf16[768,4096]{1,0:T(8,128)(2,1)} %param.8, bf16[4096,1540]{1,0:T(8,128)(2,1)} %all-gather.9.cloned.1.call-done, f32[4]{0:T(128)S(1)} %neg.9), kind=kOutput, calls=%fused_computation.89 | convolution fusion | flops 25187328 | bytes 7352336 | tf_op jit(solution)/shard_map/dot_general | solution.py:50
  111.2 1.1 reduce-window.6
  113.1 7.7 %fusion.14 = bf16[512,768]{1,0:T(8,128)(2,1)S(1)} fusion(bf16[768,4096]{1,0:T(8,128)(2,1)} %param.8, bf16[4096,1540]{1,0:T(8,128)(2,1)} %all-gather.9.cloned.1.call-done), kind=kOutput, calls=%fused_computation.20 | convolution fusion | flops 3221618688 | bytes 11272192 | tf_op jit(solution)/shard_map/dot_general | solution.py:50
  120.8 5.9 %fusion.11 = bf16[512,768]{1,0:T(8,128)(2,1)S(1)} fusion(bf16[768,4096]{1,0:T(8,128)(2,1)S(1)} %bitcast.239, bf16[4096,1540]{1,0:T(8,128)(2,1)} %all-gather.9.cloned.1.call-done), kind=kOutput, calls=%fused_computation.19 | convolution fusion | flops 3221618688 | bytes 11272192 | tf_op jit(solution)/shard_map/dot_general | solution.py:50
  127.1 2.2 all-gather
  129.3 1.8 all-gather.1
  131.1 0.8 bitcast_add_fusion.8
  132.2 11.1 %all-gather.2 = f32[8,1,4]{2,1,0:T(1,128)S(1)} all-gather(f32[1,1,4]{2,1,0:T(1,128)S(1)} %get-tuple-element.23), channel_id=1, replica_groups=mesh['seq_0'=4,'seq_1'=8,'seq_2'=2,'tp'=4] {'seq_1'}, dimensions={0}, use_global_device_ids=true | all-gather | bytes 144 | tf_op jit(solution)/shard_map/all_gather | solution.py:31
  143.4 22.0 %all-gather.11.cloned.1.call-done = f32[8,4,128,128]{3,2,1,0:T(8,128)} async-done(((f32[1,4,128,128]{3,2,1,0:T(8,128)}), f32[8,4,128,128]{3,2,1,0:T(8,128)}) %all-gather.11.cloned.1.call-update) | async-done | bytes 2097168 | tf_op jit(solution)/shard_map/all_gather | solution.py:31
  165.4 2.4 multiply_add_fusion
  168.0 7.5 %fusion.17 = bf16[512,768]{1,0:T(8,128)(2,1)S(1)} fusion(bf16[768,4096]{1,0:T(8,128)(2,1)} %param.8, bf16[4096,1540]{1,0:T(8,128)(2,1)} %all-gather.9.cloned.1.call-done), kind=kOutput, calls=%fused_computation.21 | convolution fusion | flops 3221618688 | bytes 11272192 | tf_op jit(solution)/shard_map/dot_general | solution.py:50
  175.6 7.6 %all-gather.3 = f32[4,1,4]{2,1,0:T(1,128)S(1)} all-gather(f32[1,1,4]{2,1,0:T(1,128)S(1)} %get-tuple-element.10), channel_id=1, replica_groups=mesh['seq_0'=4,'seq_1'=8,'seq_2'=2,'tp'=4] {'seq_0'}, dimensions={0}, use_global_device_ids=true | all-gather | bytes 80 | tf_op jit(solution)/shard_map/all_gather | solution.py:31
  183.6 6.6 %fusion = f32[4,128,768]{2,1,0:T(8,128)} fusion(bf16[768,4,128]{0,2,1:T(8,128)(2,1)} %bitcast.247, f32[4,768]{1,0:T(4,128)S(1)} %get-tuple-element.9, pred[768,768]{1,0:T(8,128)(4,1)S(1)} %iota_compare_fusion, bf16[768,4,128]{0,2,1:T(8,128)(2,1)S(1)} %bitcast.242, bf16[768,4,128]{0,2,1:T(8,128)(2,1)} %bitcast.249), kind=kOutput, calls=%fused_computation.1 | convolution fusion | flops 1219756032 | bytes 4534272 | tf_op jit(solution)/shard_map/hts,shv->thv/dot_general | solution.py:93
  190.3 5.0 %all-gather.13.cloned.1.call-done = f32[4,4,128,128]{3,2,1,0:T(8,128)} async-done(((f32[1,4,128,128]{3,2,1,0:T(8,128)}), f32[4,4,128,128]{3,2,1,0:T(8,128)}) %all-gather.13.cloned.1.call-update) | async-done | bytes 1048592 | tf_op jit(solution)/shard_map/all_gather | solution.py:31
  195.3 3.5 %fusion.10 = (f32[768,4]{0,1:T(4,128)S(1)}, f32[4,128,768]{2,1,0:T(8,128)S(1)}) fusion(f32[4,128,768]{2,1,0:T(8,128)} %fusion, bf16[768,4,128]{2,0,1:T(8,128)(2,1)S(1)} %copy.35, f32[768,4]{0,1:T(4,128)S(1)} %get-tuple-element.8, f32[4,4,128,128]{3,2,1,0:T(8,128)} %all-gather.13.cloned.1.call-done, f32[8,4,128,128]{3,2,1,0:T(8,128)} %all-gather.11.cloned.1.call-done, ...), kind=kOutput, calls=%fused_computation.14 | convolution fusion | flops 105903104 | bytes 7627022 | tf_op jit(solution)/shard_map/fys,ysu->fyu/dot_general | solution.py:79
  199.0 0.5 copy.39
  199.5 1.1 multiply_convert_fusion
  200.6 44.4 %all-gather.15.cloned.1.call-done = bf16[4,768,512]{2,1,0:T(8,128)(2,1)} async-done(((bf16[1,768,512]{2,1,0:T(8,128)(2,1)}), bf16[4,768,512]{2,1,0:T(8,128)(2,1)}) %all-gather.15.cloned.1.call-update) | async-done | bytes 3145744 | tf_op jit(solution)/shard_map/all_gather | solution.py:103
  245.0 3.2 %copy.40 = bf16[4,768,512]{1,2,0:T(8,128)(2,1)S(1)} copy(bf16[4,768,512]{2,1,0:T(8,128)(2,1)} %all-gather.15.cloned.1.call-done) | data formatting | bytes 6291456 | tf_op jit(solution)/shard_map/all_gather | solution.py:103
  248.2 6.8 %convolution_convert_fusion = bf16[768,1024]{1,0:T(8,128)(2,1)} fusion(bf16[768,2048]{0,1:T(8,128)(2,1)S(1)} %bitcast.240, bf16[2048,1024]{1,0:T(8,128)(2,1)} %param.15), kind=kOutput, calls=%fused_computation.11 | convolution fusion | flops 3222011904 | bytes 8912896 | tf_op jit(solution)/shard_map/dot_general | solution.py:102
  (37 shorter events, 2.3 us)
Async XLA Ops:
  6.5 99.7 %all-gather.9.cloned.1.call-start = ((), (), s32[]{:S(2)}) async-start(), calls=%async_computation | async-start | bytes 13844480 | tf_op jit(solution)/shard_map/all_gather | solution.py:13
  8.9 156.4 %all-gather.11.cloned.1.call-start = ((), (), s32[]{:S(2)}) async-start(), calls=%async_computation.1 | async-start | bytes 2359296 | tf_op jit(solution)/shard_map/all_gather | solution.py:31
  106.2 14.6 %slice-start = ((s8[6291456]{0:T(1024)(128)(4,1)}), s8[2097152]{0:T(1024)(128)(4,1)S(1)}, s32[]{:S(2)}) async-start(s8[6291456]{0:T(1024)(128)(4,1)} %bitcast.238), calls=%async_computation.4 | async-start | bytes 4194304
  113.1 7.7 %slice-start.1 = ((s8[6291456]{0:T(1024)(128)(4,1)}), s8[4194304]{0:T(1024)(128)(4,1)S(1)}, s32[]{:S(2)}) async-start(s8[6291456]{0:T(1024)(128)(4,1)} %bitcast.238), calls=%async_computation.5 | async-start | bytes 8388608
  120.8 6.0 %copy-start.1 = (bf16[512,768]{1,0:T(8,128)(2,1)}, bf16[512,768]{1,0:T(8,128)(2,1)S(1)}, u32[]{:S(2)}) copy-start(bf16[512,768]{1,0:T(8,128)(2,1)S(1)} %fusion.14) | copy-start | bytes 2359300
  126.7 4.4 %copy-start.2 = (bf16[512,768]{1,0:T(8,128)(2,1)}, bf16[512,768]{1,0:T(8,128)(2,1)S(1)}, u32[]{:S(2)}) copy-start(bf16[512,768]{1,0:T(8,128)(2,1)S(1)} %fusion.11) | copy-start | bytes 2359300
  131.9 63.4 %all-gather.13.cloned.1.call-start = ((), (), s32[]{:S(2)}) async-start(), calls=%async_computation.2 | async-start | bytes 1310720 | tf_op jit(solution)/shard_map/all_gather | solution.py:31
  167.8 77.2 %all-gather.15.cloned.1.call-start = ((), (), s32[]{:S(2)}) async-start(), calls=%async_computation.3 | async-start | bytes 3932160 | tf_op jit(solution)/shard_map/all_gather | solution.py:103
  198.8 0.7 copy-start
Sparse Core Ops, SparseCore 0:
  10.1 96.0 all-gather.8
  132.1 33.2 all-gather.10
  167.9 27.3 all-gather.12
  200.7 44.2 all-gather.14
